TPU v7x, 32 devices: a whole 2x2x4 slice. The times are simulated.
32 devices in a mesh: tp: 8 (over z, core), fs: 4 (over y, x).
Axes of the slice: x: 2, y: 2, z: 4, core: 2. Of those that a mesh axis runs over, the one named last changes fastest.
Arguments:
- tokens: bfloat16 [128, 8192], P(('tp', 'fs')), may hold values from -6 to 6
- gate_weight: bfloat16 [8192, 29568], P('fs', 'tp'), may hold values from -0.0625 to 0.0625
- up_weight: bfloat16 [8192, 29568], P('fs', 'tp'), may hold values from -0.0625 to 0.0625
- down_weight: bfloat16 [29568, 8192], P('tp', 'fs'), may hold values from -0.046875 to 0.046875
Outputs:
- mixed: bfloat16 [128, 8192], P(None, ('fs', 'tp'))
All inputs are finite; a program needn't handle non-finite values.
Results may differ from a plain program's by a relative error of at most 0.0049.
Values may be sent and summed in bfloat16 or wider, within the bound.
A program may use at most 128 MiB of HBM per device.

v0:
```python
import jax
import jax.numpy as jnp
from jax import lax
from jax.sharding import PartitionSpec as P


def body(tokens, gate_weight, up_weight, down_weight):
    by_feature = lax.all_to_all(tokens, "fs", split_axis=1, concat_axis=0, tiled=True)
    feature_rows = lax.all_gather(by_feature, "tp", axis=0, tiled=True)
    gate_part = jnp.dot(feature_rows, gate_weight, preferred_element_type=jnp.float32)
    up_part = jnp.dot(feature_rows, up_weight, preferred_element_type=jnp.float32)
    gate, up = (
        lax.psum_scatter(gate_part, "fs", scatter_dimension=1, tiled=True),
        lax.psum_scatter(up_part, "fs", scatter_dimension=1, tiled=True),
    )
    hidden = (jax.nn.silu(gate) * up).astype(jnp.bfloat16)
    hidden_all = lax.all_gather(hidden, "fs", axis=1, tiled=True)
    partial_out = jnp.dot(hidden_all, down_weight, preferred_element_type=jnp.float32)
    summed = lax.psum_scatter(partial_out, "tp", scatter_dimension=1, tiled=True)
    return summed.astype(jnp.bfloat16)


def solution(mesh):
    return jax.shard_map(
        body,
        mesh=mesh,
        in_specs=(P(("tp", "fs"), None), P("fs", "tp"), P("fs", "tp"), P("tp", "fs")),
        out_specs=P(None, ("fs", "tp")),
        check_vma=False,
    )
```

profile of v0, /device:TPU:0, one launch (start us, length us, event | category | flops | bytes accessed | tf_op | source)
XLA Modules:
  0.0 184.2 jit_solution(5929641926974322343)
XLA Ops:
  6.5 0.0 reduce-scatter.6.cloned.1.call-start
  6.5 10.0 %all_to_all.19 = bf16[4,4,2048]{2,0,1:T(4,128)(2,1)S(1)} all-to-all(bf16[4,4,2048]{2,0,1:T(4,128)(2,1)} %bitcast.19), channel_id=1, replica_groups=mesh['tp'=8,'fs'=4] {'fs'}, dimensions={1} | all-to-all | bytes 131072 | tf_op jit(solution)/shard_map/all_to_all | solution.py:8
  16.6 0.0 copy-start
  16.6 15.1 %all_gather.6 = bf16[128,2048]{1,0:T(8,128)(2,1)S(1)} all-gather(bf16[16,2048]{1,0:T(8,128)(2,1)S(1)} %all_to_all.17), channel_id=1, replica_groups=mesh['tp'=8,'fs'=4] {'tp'}, dimensions={0}, use_global_device_ids=true | all-gather | bytes 589824 | tf_op jit(solution)/shard_map/all_gather | solution.py:9
  31.8 7.6 %fusion.5 = f32[128,3696]{0,1:T(8,128)S(1)} fusion(bf16[128,2048]{1,0:T(8,128)(2,1)S(1)} %all_gather.6, bf16[2048,3696]{0,1:T(8,128)(2,1)} %param.5), kind=kOutput, calls=%fused_computation.3 | convolution fusion | flops 1937768448 | bytes 17555456 | tf_op jit(solution)/shard_map/dot_general | solution.py:10
  39.3 0.0 copy-done
  39.3 0.0 copy-start.1
  39.4 5.6 %fusion.6 = f32[128,3696]{0,1:T(8,128)} fusion(bf16[128,2048]{1,0:T(8,128)(2,1)S(1)} %all_gather.6, bf16[2048,3696]{0,1:T(8,128)(2,1)S(1)} %copy-done), kind=kOutput, calls=%fused_computation.4 | convolution fusion | flops 1937768448 | bytes 17555456 | tf_op jit(solution)/shard_map/dot_general | solution.py:11
  44.9 67.6 %fusion.4 = (f32[128,928]{0,1:T(8,128)S(1)}, f32[128,928]{0,1:T(8,128)S(1)}) fusion(f32[128,3696]{0,1:T(8,128)} %fusion.6, f32[128,3696]{0,1:T(8,128)S(1)} %fusion.5), kind=kCustom, calls=%all-reduce-scatter.2 | all-reduce-scatter fusion | flops 950273 | bytes 4735488
  112.6 1.7 collective-permute-start
  114.3 4.3 %collective-permute-start.1 = (f32[128,12]{0,1:T(8,128)S(1)}, f32[128,12]{0,1:T(8,128)S(1)}, u32[]{:S(2)}, u32[]{:S(2)}) collective-permute-start(f32[128,12]{0,1:T(8,128)S(1)} %slice.1), channel_id=1, source_target_pairs={{0,1},{1,2},{2,3},{4,5},{5,6},{6,7},{8,9},{9,10},{10,11},{12,13},{... | collective-permute-start | bytes 18440
  118.6 0.0 copy-done.1
  118.6 0.6 dynamic-slice.6
  119.9 0.0 collective-permute-done
  119.9 1.1 concatenate
  121.0 0.0 collective-permute-done.1
  121.0 1.1 concatenate.1
  122.1 0.2 fusion.3
  122.3 12.0 %all-gather = bf16[4,924,128]{2,1,0:T(8,128)(2,1)S(1)} all-gather(bf16[1,924,128]{2,1,0:T(8,128)(2,1)S(1)} %fusion.3), channel_id=1, replica_groups=mesh['tp'=8,'fs'=4] {'fs'}, dimensions={0}, use_global_device_ids=true | all-gather | bytes 1182720 | tf_op jit(solution)/shard_map/all_gather | solution.py:17
  134.3 0.2 reshape.4
  134.5 8.5 %fusion.7 = f32[128,2048]{1,0:T(8,128)} fusion(bf16[3696,128]{1,0:T(8,128)(2,1)S(1)} %reshape.4, bf16[3696,2048]{1,0:T(8,128)(2,1)} %param.7), kind=kOutput, calls=%fused_computation.5 | convolution fusion | flops 1937768448 | bytes 17133568 | tf_op jit(solution)/shard_map/dot_general | solution.py:18
  143.0 0.0 reduce-scatter.6.cloned.1.call-update
  143.0 32.8 %reduce-scatter.6.cloned.1.call-done = f32[128,256]{1,0:T(8,128)} async-done(((f32[128,2048]{1,0:T(8,128)}), f32[128,256]{1,0:T(8,128)}) %reduce-scatter.6.cloned.1.call-update) | async-done | bytes 131088 | tf_op jit(solution)/shard_map/reduce_scatter | solution.py:19
  175.8 1.5 convert_element_type.7
  (3 shorter events, 0.0 us)
Async XLA Ops:
  6.5 169.3 %reduce-scatter.6.cloned.1.call-start = ((), (), s32[]{:S(2)}) async-start(), calls=%async_computation.2 | async-start | bytes 1179648 | tf_op jit(solution)/shard_map/reduce_scatter | solution.py:19
  16.6 22.7 %copy-start = (bf16[2048,3696]{0,1:T(8,128)(2,1)S(1)}, bf16[2048,3696]{0,1:T(8,128)(2,1)}, u32[]{:S(2)}) copy-start(bf16[2048,3696]{0,1:T(8,128)(2,1)} %param.6) | copy-start | bytes 45416452
  39.3 79.3 %copy-start.1 = (u32[32]{0:T(128)S(1)}, u32[32]{0:T(128)}, u32[]{:S(2)}) copy-start(u32[32]{0:T(128)} %constant.6) | copy-start | bytes 388
  112.6 7.3 %collective-permute-start = (f32[128,12]{0,1:T(8,128)S(1)}, f32[128,12]{0,1:T(8,128)S(1)}, u32[]{:S(2)}, u32[]{:S(2)}) collective-permute-start(f32[128,12]{0,1:T(8,128)S(1)} %slice), channel_id=1, source_target_pairs={{0,1},{1,2},{2,3},{4,5},{5,6},{6,7},{8,9},{9,10},{10,11},{12,13},{... | collective-permute-start | bytes 18440
  114.3 6.7 %collective-permute-start.1 = (f32[128,12]{0,1:T(8,128)S(1)}, f32[128,12]{0,1:T(8,128)S(1)}, u32[]{:S(2)}, u32[]{:S(2)}) collective-permute-start(f32[128,12]{0,1:T(8,128)S(1)} %slice.1), channel_id=1, source_target_pairs={{0,1},{1,2},{2,3},{4,5},{5,6},{6,7},{8,9},{9,10},{10,11},{12,13},{... | collective-permute-start | bytes 18440
Sparse Core Ops, SparseCore 0:
  143.1 32.6 reduce-scatter.5
where the time goes:
time: 185 us; the launch traced here: 184 us
  blocking collectives  105 us (57%)
  waiting for transfers between devices  32.9 us (18%)
  matrix products  21.6 us (12%)
  between operations  14.2 us (8%)
  starting transfers between devices  6.01 us (3%)
  local copies, waits for them, and re-layouts  3.02 us (2%)
    unnamed x1, blocking collectives  67.6 us
    reduce_scatter x1, waiting for transfers between devices, body(): lax.psum_scatter(partial_out, 'tp', scatter_dimension=1, tiled=True)  32.8 us
    all_gather x1, blocking collectives, body(): feature_rows = lax.all_gather(by_feature, 'tp', axis=0, tiled=True)  15.1 us
    all_gather x1, blocking collectives, body(): hidden_all = lax.all_gather(hidden, 'fs', axis=1, tiled=True)  12 us
    all_to_all x1, blocking collectives, body(): lax.all_to_all(tokens, 'fs', split_axis=1, concat_axis=0, tiled=True)  10 us
    dot_general x1, matrix products, body(): jnp.dot(hidden_all, down_weight, preferred_element_type=jnp.float32)  8.5 us
    dot_general x1, matrix products, body(): jnp.dot(feature_rows, gate_weight, preferred_element_type=jnp.float32)  7.58 us
    unnamed x2, starting transfers between devices  6.01 us
  transfers between devices with their start and end apart: 3, of which 1 were waited for; matrix products, arithmetic and copies ran while one was open for 1% of the time, Pallas kernels for 0%

commit v1 on v0

--- a/solution.py
+++ b/solution.py
@@ -14,7 +14,8 @@
         lax.psum_scatter(up_part, "fs", scatter_dimension=1, tiled=True),
     )
     hidden = (jax.nn.silu(gate) * up).astype(jnp.bfloat16)
-    hidden_all = lax.all_gather(hidden, "fs", axis=1, tiled=True)
+    parts = lax.all_gather(hidden, "fs", axis=0, tiled=False)
+    hidden_all = jnp.concatenate(parts, axis=1)
     partial_out = jnp.dot(hidden_all, down_weight, preferred_element_type=jnp.float32)
     summed = lax.psum_scatter(partial_out, "tp", scatter_dimension=1, tiled=True)
     return summed.astype(jnp.bfloat16)

time: 185 us -> 185 us (level)
  no operation moved by 1% of the time
where the time goes in v1:
time: 185 us
  blocking collectives  105 us (57%)
  waiting for transfers between devices  33.2 us (18%)
  matrix products  21.6 us (12%)
  between operations  14.2 us (8%)
  starting transfers between devices  6.01 us (3%)
  local copies, waits for them, and re-layouts  3.47 us (2%)
    unnamed x1, blocking collectives  67.6 us
    reduce_scatter x1, waiting for transfers between devices, body(): lax.psum_scatter(partial_out, 'tp', scatter_dimension=1, tiled=True)  33.2 us
    all_gather x1, blocking collectives, body(): feature_rows = lax.all_gather(by_feature, 'tp', axis=0, tiled=True)  15.1 us
    all_gather x1, blocking collectives, body(): parts = lax.all_gather(hidden, 'fs', axis=0, tiled=False)  12 us
    all_to_all x1, blocking collectives, body(): lax.all_to_all(tokens, 'fs', split_axis=1, concat_axis=0, tiled=True)  10 us
    dot_general x1, matrix products, body(): jnp.dot(hidden_all, down_weight, preferred_element_type=jnp.float32)  8.5 us
    dot_general x1, matrix products, body(): jnp.dot(feature_rows, gate_weight, preferred_element_type=jnp.float32)  7.58 us
    unnamed x2, starting transfers between devices  6.01 us
  transfers between devices with their start and end apart: 3, of which 1 were waited for; matrix products, arithmetic and copies ran while one was open for 1% of the time, Pallas kernels for 0%

profile of v1, /device:TPU:0, one launch (start us, length us, event | category | flops | bytes accessed | tf_op | source)
XLA Modules:
  0.0 185.0 jit_solution(5485690145713021485)
XLA Ops:
  6.5 0.0 reduce-scatter.6.cloned.1.call-start
  6.5 10.0 %all_to_all.19 = bf16[4,4,2048]{2,0,1:T(4,128)(2,1)S(1)} all-to-all(bf16[4,4,2048]{2,0,1:T(4,128)(2,1)} %bitcast.23), channel_id=1, replica_groups=mesh['tp'=8,'fs'=4] {'fs'}, dimensions={1} | all-to-all | bytes 131072 | tf_op jit(solution)/shard_map/all_to_all | solution.py:8
  16.6 0.0 copy-start
  16.6 15.1 %all_gather.9 = bf16[128,2048]{1,0:T(8,128)(2,1)S(1)} all-gather(bf16[16,2048]{1,0:T(8,128)(2,1)S(1)} %all_to_all.17), channel_id=1, replica_groups=mesh['tp'=8,'fs'=4] {'tp'}, dimensions={0}, use_global_device_ids=true | all-gather | bytes 589824 | tf_op jit(solution)/shard_map/all_gather | solution.py:9
  31.8 7.6 %fusion.4 = f32[128,3696]{0,1:T(8,128)S(1)} fusion(bf16[128,2048]{1,0:T(8,128)(2,1)S(1)} %all_gather.9, bf16[2048,3696]{0,1:T(8,128)(2,1)} %param.5), kind=kOutput, calls=%fused_computation.3 | convolution fusion | flops 1937768448 | bytes 17555456 | tf_op jit(solution)/shard_map/dot_general | solution.py:10
  39.3 0.0 copy-done
  39.3 0.0 copy-start.1
  39.4 5.6 %fusion.5 = f32[128,3696]{0,1:T(8,128)} fusion(bf16[128,2048]{1,0:T(8,128)(2,1)S(1)} %all_gather.9, bf16[2048,3696]{0,1:T(8,128)(2,1)S(1)} %copy-done), kind=kOutput, calls=%fused_computation.4 | convolution fusion | flops 1937768448 | bytes 17555456 | tf_op jit(solution)/shard_map/dot_general | solution.py:11
  44.9 67.6 %fusion.3 = (f32[128,928]{0,1:T(8,128)S(1)}, f32[128,928]{0,1:T(8,128)S(1)}) fusion(f32[128,3696]{0,1:T(8,128)} %fusion.5, f32[128,3696]{0,1:T(8,128)S(1)} %fusion.4), kind=kCustom, calls=%all-reduce-scatter.2 | all-reduce-scatter fusion | flops 950273 | bytes 4735488
  112.6 1.7 collective-permute-start
  114.3 4.3 %collective-permute-start.1 = (f32[128,12]{0,1:T(8,128)S(1)}, f32[128,12]{0,1:T(8,128)S(1)}, u32[]{:S(2)}, u32[]{:S(2)}) collective-permute-start(f32[128,12]{0,1:T(8,128)S(1)} %slice.1), channel_id=1, source_target_pairs={{0,1},{1,2},{2,3},{4,5},{5,6},{6,7},{8,9},{9,10},{10,11},{12,13},{... | collective-permute-start | bytes 18440
  118.6 0.0 copy-done.1
  118.6 0.6 dynamic-slice.6
  119.9 0.0 collective-permute-done
  119.9 1.1 concatenate
  121.0 0.0 collective-permute-done.1
  121.0 1.1 concatenate.1
  122.1 0.2 fusion.2
  122.3 12.0 %all-gather = bf16[512,924]{0,1:T(8,128)(2,1)S(1)} all-gather(bf16[128,924]{0,1:T(8,128)(2,1)S(1)} %fusion.2), channel_id=2, replica_groups=mesh['tp'=8,'fs'=4] {'fs'}, dimensions={0}, use_global_device_ids=true | all-gather | bytes 1182720 | tf_op jit(solution)/shard_map/all_gather | solution.py:17
  134.3 0.3 reshape.11
  134.6 0.1 copy.10
  134.8 0.2 reshape.10
  134.9 8.5 %fusion.6 = f32[128,2048]{1,0:T(8,128)} fusion(bf16[128,3696]{0,1:T(8,128)(2,1)S(1)} %reshape.10, bf16[3696,2048]{1,0:T(8,128)(2,1)} %param.7), kind=kOutput, calls=%fused_computation.5 | convolution fusion | flops 1937768448 | bytes 17133568 | tf_op jit(solution)/shard_map/dot_general | solution.py:19
  143.4 0.0 reduce-scatter.6.cloned.1.call-update
  143.5 33.2 %reduce-scatter.6.cloned.1.call-done = f32[128,256]{1,0:T(8,128)} async-done(((f32[128,2048]{1,0:T(8,128)}), f32[128,256]{1,0:T(8,128)}) %reduce-scatter.6.cloned.1.call-update) | async-done | bytes 131088 | tf_op jit(solution)/shard_map/reduce_scatter | solution.py:20
  176.6 1.5 convert_element_type.7
  (3 shorter events, 0.0 us)
Async XLA Ops:
  6.5 170.1 %reduce-scatter.6.cloned.1.call-start = ((), (), s32[]{:S(2)}) async-start(), calls=%async_computation.2 | async-start | bytes 1179648 | tf_op jit(solution)/shard_map/reduce_scatter | solution.py:20
  16.6 22.7 %copy-start = (bf16[2048,3696]{0,1:T(8,128)(2,1)S(1)}, bf16[2048,3696]{0,1:T(8,128)(2,1)}, u32[]{:S(2)}) copy-start(bf16[2048,3696]{0,1:T(8,128)(2,1)} %param.6) | copy-start | bytes 45416452
  39.3 79.3 %copy-start.1 = (u32[32]{0:T(128)S(1)}, u32[32]{0:T(128)}, u32[]{:S(2)}) copy-start(u32[32]{0:T(128)} %constant.6) | copy-start | bytes 388
  112.6 7.3 %collective-permute-start = (f32[128,12]{0,1:T(8,128)S(1)}, f32[128,12]{0,1:T(8,128)S(1)}, u32[]{:S(2)}, u32[]{:S(2)}) collective-permute-start(f32[128,12]{0,1:T(8,128)S(1)} %slice), channel_id=1, source_target_pairs={{0,1},{1,2},{2,3},{4,5},{5,6},{6,7},{8,9},{9,10},{10,11},{12,13},{... | collective-permute-start | bytes 18440
  114.3 6.7 %collective-permute-start.1 = (f32[128,12]{0,1:T(8,128)S(1)}, f32[128,12]{0,1:T(8,128)S(1)}, u32[]{:S(2)}, u32[]{:S(2)}) collective-permute-start(f32[128,12]{0,1:T(8,128)S(1)} %slice.1), channel_id=1, source_target_pairs={{0,1},{1,2},{2,3},{4,5},{5,6},{6,7},{8,9},{9,10},{10,11},{12,13},{... | collective-permute-start | bytes 18440
Sparse Core Ops, SparseCore 0:
  143.6 33.0 reduce-scatter.5
